TPU v7x, 256 devices: a whole 4x4x8 slice. The times are simulated.
256 devices in a mesh: grow: 16 (over y_lo, x, core), gcol: 16 (over z, y_hi).
Axes of the slice: x: 4, y: 4 (y_hi: 2, y_lo: 2; y = y_hi * 2 + y_lo), z: 8, core: 2. Of those that a mesh axis runs over, the one named last changes fastest.
Arguments:
- eps_static: float32 [12288, 12288], P('grow', 'gcol'), may hold values from -1.8 to 1.8
- eps_imag: float32 [12288, 12288], P('grow', 'gcol'), may hold values from -1.8 to 1.8
- frequency_grid: float32 [3], replicated, may hold values from 0.1 to 2
- band_energy: float32 [32], replicated, may hold values from -2 to 2
- pair_elements: bfloat16 [32, 64, 12288], P('grow', None, 'gcol'), may hold values from -0.0546875 to 0.0546875
Outputs:
- sigma: float32 [3, 64], P(None, 'gcol')
All inputs are finite; a program needn't handle non-finite values.
Results may differ from a plain program's by a relative error of at most 0.0019.
Values may be sent and summed in bfloat16 or wider, within the bound.
A program may use at most 64 MiB of HBM per device.

v0:
```python
import jax
import jax.numpy as jnp
from jax import lax
from jax.sharding import Mesh
from jax.sharding import PartitionSpec as P

NE = 3
GROW = ("grow_0", "grow_1", "grow_2")
GCOL = ("gcol_0", "gcol_1")


def gathered_by_axis(shard, axes, dim):
    for axis in reversed(axes):
        shard = lax.all_gather(shard, axis, axis=dim, tiled=True)
    return shard


def split_up(shard, dim, devices):
    lengths = shard.shape
    parts = shard.reshape(*lengths[:dim], devices, lengths[dim] // devices, *lengths[dim + 1 :])
    return jnp.moveaxis(parts, dim, 0)


def joined_along(parts, dim):
    lengths = list(parts.shape[1:])
    lengths[dim] *= parts.shape[0]
    return jnp.moveaxis(parts, 0, dim).reshape(lengths)


def turned_blocks(parts, axes, order):
    inside = parts.shape[1:]
    out = parts.reshape(*(lax.axis_size(a) for a in axes), *inside)
    for k in order:
        out = lax.all_to_all(out, axes[k], k, k, tiled=True)
    return out.reshape(-1, *inside)


def core_and_chips(shard, groups, order, split_dim, concat_dim):
    devices = lax.axis_size(groups[0]) * lax.axis_size(groups[1])
    parts = split_up(shard, split_dim, devices)
    return joined_along(turned_blocks(parts, groups, order), concat_dim)


def summed_on_arrival(shard, axis, dim):
    devices = lax.axis_size(axis)
    parts = lax.all_to_all(split_up(shard, dim, devices), axis, 0, 0, tiled=True)
    return jnp.sum(parts, axis=0)


def from_everyone(shard, axis):
    copies = jnp.broadcast_to(shard, (lax.axis_size(axis), *shard.shape))
    return lax.all_to_all(copies, axis, split_axis=0, concat_axis=0, tiled=True)


def of_everyone(shard, axis):
    everything = from_everyone(shard, axis)
    return jnp.sum(everything, axis=0)


def shards(eps_static, eps_imag, frequency_grid, band_energy, pair_elements):
    row_count = lax.axis_size(GROW)
    row_index = lax.axis_index(GROW)
    col_index = lax.axis_index(GCOL)
    height = eps_static.shape[0]
    breadth = eps_static.shape[1]
    bands = pair_elements.shape[0] * row_count
    states = pair_elements.shape[1]
    column_panel = lax.all_gather(pair_elements, GROW, axis=0, tiled=True)
    own_bands = gathered_by_axis(pair_elements, GCOL, 2)
    row_panel = core_and_chips(own_bands, (("grow_0", "grow_1"), "grow_2"), (1, 0), 2, 0)
    global_rows = row_index * height + lax.iota(jnp.int32, height)
    global_cols = col_index * breadth + lax.iota(jnp.int32, breadth)
    kronecker = (global_rows[:, None] == global_cols[None, :]).astype(jnp.float32)
    static_part = eps_static - kronecker
    imag_part = eps_imag - kronecker
    spread = static_part - imag_part
    pole_square = (imag_part * imag_part + 0.25) / (spread * spread + 0.25)
    pole_freq = jnp.sqrt(pole_square)
    strength = -static_part * pole_square
    left_rows = row_panel.reshape(bands * states, height)
    right_rows = column_panel.reshape(bands * states, breadth)
    terms = []
    for point in range(NE):
        kernel = (strength / (pole_freq * (pole_freq + frequency_grid[point]))).astype(jnp.bfloat16)
        projected = jnp.dot(left_rows, kernel, preferred_element_type=jnp.float32)
        terms.append(jnp.sum(projected * right_rows, axis=1))
    quad = jnp.stack(terms).reshape(NE, bands, states)
    offset_energy = frequency_grid[:, None] - band_energy[None, :]
    weight = 1.0 / (1.0 + offset_energy * offset_energy)
    partial_sigma = jnp.einsum("em,ems->es", weight, quad)
    shares = summed_on_arrival(partial_sigma, GCOL, 1)
    return of_everyone(shares, GROW)


def solution(mesh):
    finer = Mesh(
        mesh.devices.reshape(2, 4, 2, 8, 2), ("grow_0", "grow_1", "grow_2", "gcol_0", "gcol_1")
    )
    in_specs = (P(GROW, GCOL), P(GROW, GCOL), P(), P(), P(GROW, None, GCOL))
    out_specs = P(None, GCOL)
    return jax.shard_map(
        shards, mesh=finer, in_specs=in_specs, out_specs=out_specs, check_vma=False
    )
```

profile of v0, /device:TPU:1, one launch (start us, length us, event | category | flops | bytes accessed | tf_op | source)
XLA Modules:
  0.0 211.0 jit_solution(8430354224616254626)
XLA Ops:
  6.5 0.0 all-gather.3.cloned.1.call-start
  6.5 10.5 %all_gather.9 = bf16[2,64,1536]{2,1,0:T(8,128)(2,1)} all-gather(bf16[2,64,768]{2,1,0:T(8,128)(2,1)} %param.9), channel_id=1, replica_groups=mesh['grow_0'=2,'grow_1'=4,'grow_2'=2,'gcol_0'=8,'gcol_1'=2] {'gcol_1'}, dimensions={2}, use_global_device_ids=true | all-gather | bytes 589824 | tf_op jit(solution)/shard_map/all_gather | solution.py:14
  17.0 0.0 all-gather.3.cloned.1.call-update
  17.0 0.0 all-gather.5.cloned.1.call-start
  17.1 0.7 all-gather.5.cloned.1.call-update
  17.8 46.2 %all-gather.3.cloned.1.call-done = bf16[2,64,12288]{2,1,0:T(8,128)(2,1)} async-done(((bf16[2,64,1536]{2,1,0:T(8,128)(2,1)}), bf16[2,64,12288]{2,1,0:T(8,128)(2,1)}) %all-gather.3.cloned.1.call-update) | async-done | bytes 3145744 | tf_op jit(solution)/shard_map/all_gather | solution.py:14
  64.0 2.7 %copy.47 = bf16[16,8,16,768]{3,2,1,0:T(8,128)(2,1)S(1)} copy(bf16[16,8,16,768]{3,1,2,0:T(8,128)(2,1)} %bitcast.42) | data formatting | bytes 6291456
  66.7 0.2 bitcast_bitcast_fusion
  66.9 1.0 copy.36
  67.9 0.3 copy.37
  68.3 7.1 %all_to_all.20 = bf16[8,2,2,64,768]{4,3,2,0,1:T(8,128)(2,1)S(1)} all-to-all(bf16[8,2,2,64,768]{4,3,2,0,1:T(8,128)(2,1)S(1)} %copy.37), channel_id=1, replica_groups=mesh['grow_0'=2,'grow_1'=4,'grow_2'=2,'gcol_0'=8,'gcol_1'=2] {'grow_2'}, dimensions={1} | all-to-all | bytes 6291456 | tf_op jit(solution)/shard_map/all_to_all | solution.py:34
  75.4 2.0 copy.38
  77.4 5.0 %all-to-all-start.1 = ((bf16[8,2,2,64,768]{4,3,2,1,0:T(8,128)(2,1)}), bf16[8,2,2,64,768]{4,3,2,1,0:T(8,128)(2,1)S(1)}, u32[]{:S(2)}, u32[]{:S(2)}) async-start(bf16[8,2,2,64,768]{4,3,2,1,0:T(8,128)(2,1)} %copy.38), calls=%async_computation.1 | async-start | bytes 6291456 | tf_op jit(solution)/shard_map/all_to_all | solution.py:34
  82.4 0.0 copy-done
  82.4 0.7 fusion.26
  83.1 0.0 copy-done.1
  83.1 0.1 divide_bitcast_fusion
  83.2 53.7 %all-gather.5.cloned.1.call-done = bf16[32,64,768]{2,1,0:T(8,128)(2,1)} async-done(((bf16[2,64,768]{2,1,0:T(8,128)(2,1)}), bf16[32,64,768]{2,1,0:T(8,128)(2,1)}) %all-gather.5.cloned.1.call-update) | async-done | bytes 3145744 | tf_op jit(solution)/shard_map/all_gather | solution.py:68
  136.8 5.0 %bitcast_convert_fusion = f32[2048,768]{1,0:T(8,128)} fusion(bf16[32,64,768]{2,1,0:T(8,128)(2,1)} %all-gather.5.cloned.1.call-done), kind=kLoop, calls=%fused_computation.12 | loop fusion | flops 1572864 | bytes 9437184 | tf_op jit(solution)/shard_map/convert_element_type | solution.py:86
  141.9 6.6 %copy.39 = f32[2048,768]{0,1:T(8,128)} copy(f32[2048,768]{1,0:T(8,128)} %bitcast_convert_fusion) | data formatting | bytes 12582912 | tf_op jit(solution)/shard_map/convert_element_type | solution.py:86
  148.5 0.0 all-to-all-done.1
  148.5 9.0 %fusion = bf16[2048]{0:T(1024)(128)(2,1)S(1)} fusion(f32[2048,768]{0,1:T(8,128)} %copy.39, bf16[2048,768]{1,0:T(8,128)(2,1)S(1)} %bitcast.39, f32[]{:T(128)} %bitcast.10, f32[768,768]{1,0:T(8,128)} %param.5, s32[768]{0:T(1024)S(1)} %get-tuple-element.8, s32[768]{0:T(1024)S(1)} %get-tuple-element.9, f32[768,768]{1,0:T(8,128)} %param.6), kind=kOutput, calls=%fused_computation.1 | convolution fusion | flops 2428499968 | bytes 14166020 | tf_op jit(solution)/shard_map/dot_general | solution.py:85
  157.5 0.1 stack.14
  157.6 9.0 %fusion.1 = bf16[2048]{0:T(1024)(128)(2,1)S(1)} fusion(f32[2048,768]{0,1:T(8,128)} %copy.39, bf16[2048,768]{1,0:T(8,128)(2,1)S(1)} %bitcast.40, f32[]{:T(128)} %bitcast.7, f32[768,768]{1,0:T(8,128)} %param.5, s32[768]{0:T(1024)S(1)} %get-tuple-element.8, s32[768]{0:T(1024)S(1)} %get-tuple-element.9, f32[768,768]{1,0:T(8,128)} %param.6), kind=kOutput, calls=%fused_computation.3 | convolution fusion | flops 2428499968 | bytes 14166020 | tf_op jit(solution)/shard_map/dot_general | solution.py:85
  166.6 0.1 stack.13
  166.7 9.0 %fusion.2 = bf16[2048]{0:T(1024)(128)(2,1)S(1)} fusion(f32[2048,768]{0,1:T(8,128)} %copy.39, bf16[2048,768]{1,0:T(8,128)(2,1)S(1)} %bitcast.41, f32[]{:T(128)} %bitcast.1, f32[768,768]{1,0:T(8,128)} %param.5, s32[768]{0:T(1024)S(1)} %get-tuple-element.8, s32[768]{0:T(1024)S(1)} %get-tuple-element.9, f32[768,768]{1,0:T(8,128)} %param.6), kind=kOutput, calls=%fused_computation.5 | convolution fusion | flops 2428499968 | bytes 14166020 | tf_op jit(solution)/shard_map/dot_general | solution.py:85
  175.7 0.1 stack.12
  175.8 0.1 fusion.18
  175.9 0.1 reshape.31
  176.0 17.6 %all_to_all.21 = f32[16,3,4]{2,1,0:T(4,128)S(1)} all-to-all(f32[16,3,4]{2,1,0:T(4,128)S(1)} %copy.42), channel_id=1, replica_groups=mesh['grow_0'=2,'grow_1'=4,'grow_2'=2,'gcol_0'=8,'gcol_1'=2] {'gcol_0','..., dimensions={0} | all-to-all | bytes 1536 | tf_op jit(solution)/shard_map/all_to_all | solution.py:46
  193.6 9.9 %all_to_all.22 = f32[16,3,4]{2,1,0:T(4,128)S(1)} all-to-all(f32[16,3,4]{2,1,0:T(4,128)S(1)} %broadcast_in_dim.2), channel_id=1, replica_groups=mesh['grow_0'=2,'grow_1'=4,'grow_2'=2,'gcol_0'=8,'gcol_1'=2] {'grow_0','..., dimensions={0} | all-to-all | bytes 1536 | tf_op jit(solution)/shard_map/all_to_all | solution.py:52
  203.5 0.6 reduce_sum.49
  (7 shorter events, 0.1 us)
Async XLA Ops:
  6.5 57.5 %all-gather.3.cloned.1.call-start = ((), (), s32[]{:S(2)}) async-start(), calls=%async_computation.4 | async-start | bytes 3538944 | tf_op jit(solution)/shard_map/all_gather | solution.py:14
  17.0 119.8 %all-gather.5.cloned.1.call-start = ((), (), s32[]{:S(2)}) async-start(), calls=%async_computation.5 | async-start | bytes 3342336 | tf_op jit(solution)/shard_map/all_gather | solution.py:68
  77.4 5.0 %copy-start = (f32[3]{0:T(128)S(1)}, f32[3]{0:T(128)}, u32[]{:S(2)}) copy-start(f32[3]{0:T(128)} %param.7) | copy-start | bytes 40
  77.4 5.7 %copy-start.1 = (f32[32]{0:T(128)S(1)}, f32[32]{0:T(128)}, u32[]{:S(2)}) copy-start(f32[32]{0:T(128)} %param.8) | copy-start | bytes 388
  77.4 71.1 %all-to-all-start.1 = ((bf16[8,2,2,64,768]{4,3,2,1,0:T(8,128)(2,1)}), bf16[8,2,2,64,768]{4,3,2,1,0:T(8,128)(2,1)S(1)}, u32[]{:S(2)}, u32[]{:S(2)}) async-start(bf16[8,2,2,64,768]{4,3,2,1,0:T(8,128)(2,1)} %copy.38), calls=%async_computation.1 | async-start | bytes 6291456 | tf_op jit(solution)/shard_map/all_to_all | solution.py:34
Sparse Core Ops, SparseCore 0:
  17.2 46.8 all-gather.2
  65.9 70.9 all-gather.4
where the time goes:
time: 211 us
  waiting for transfers between devices  101 us (48%)
  blocking collectives  45.1 us (21%)
  matrix products  27.1 us (13%)
  local copies, waits for them, and re-layouts  13.8 us (7%)
  between operations  13.5 us (6%)
  other arithmetic  5.74 us (3%)
  starting transfers between devices  5.07 us (2%)
    all_gather x1, waiting for transfers between devices, shards(): column_panel = lax.all_gather(pair_elements, GROW, axis=0, tiled=True)  53.7 us
    all_gather x1, waiting for transfers between devices, gathered_by_axis(): shard = lax.all_gather(shard, axis, axis=dim, tiled=True)  46.2 us
    dot_general x3, matrix products, shards(): projected = jnp.dot(left_rows, kernel, preferred_element_type=jnp.float32)  27 us
    all_to_all x1, blocking collectives, summed_on_arrival(): lax.all_to_all(split_up(shard, dim, devices), axis, 0, 0, tiled=True)  17.6 us
    all_gather x1, blocking collectives, gathered_by_axis(): shard = lax.all_gather(shard, axis, axis=dim, tiled=True)  10.5 us
    all_to_all x1, blocking collectives, from_everyone(): return lax.all_to_all(copies, axis, split_axis=0, concat_axis=0, tiled=True)  9.92 us
    all_to_all x1, blocking collectives, turned_blocks(): out = lax.all_to_all(out, axes[k], k, k, tiled=True)  7.13 us
    convert_element_type x1, local copies, waits for them, and re-layouts, shards(): terms.append(jnp.sum(projected * right_rows, axis=1))  6.6 us
  transfers between devices with their start and end apart: 3, of which 2 were waited for; matrix products, arithmetic and copies ran while one was open for 9% of the time, Pallas kernels for 0%

commit v1 on v0

v1 whole, which is shorter than its diff:
```python
import jax
import jax.numpy as jnp
from jax import lax
from jax.experimental import pallas as pl
from jax.experimental.pallas import tpu as pltpu
from jax.sharding import Mesh
from jax.sharding import PartitionSpec as P

NE = 3
NX = 4
NZ = 8
GROW = ("grow_0", "grow_1", "grow_2")
GCOL = ("gcol_0", "gcol_1")
MESH = pl.DeviceIdType.MESH
PEERS = ((0, 1), (0, 3), (1, 0), (1, 1), (1, 3), (0, 2), (1, 2))
SLICE = 16


def kernel(
    static_hbm, imag_hbm, freq, band, pair_hbm, out,
    rowp, colp, kmat, stat, imag, acc, red1, red2,
    in_sem, row_recv, row_send, col_recv, col_send, r1_recv, r1_send, r2_recv, r2_send,
):
    ylo, x, core = (lax.axis_index(a) for a in GROW)
    z, yhi = (lax.axis_index(a) for a in GCOL)
    plane = 4 * ylo + x
    row = plane * 2 + core
    col = z * 2 + yhi
    own_source = jnp.logical_and(plane == z, core == yhi)

    loads = [
        pltpu.make_async_copy(pair_hbm, colp.at[row], in_sem.at[0]),
        pltpu.make_async_copy(static_hbm, stat, in_sem.at[1]),
        pltpu.make_async_copy(imag_hbm, imag, in_sem.at[2]),
    ]
    for load in loads:
        load.start()

    barrier = pltpu.get_barrier_semaphore()

    def greet(device):
        pl.semaphore_signal(barrier, inc=1, device_id=device, device_id_type=MESH)

    for k in range(2):
        @pl.when(jnp.logical_not(jnp.logical_and(plane == z, jnp.logical_and(core == yhi, core == k))))
        def _():
            greet((z // NX, z % NX, k, plane, core))

    @pl.loop(1, 16)
    def _(i):
        dz, dh = i // 2, i % 2
        greet((ylo, x, core, (z + dz) % NZ, (yhi + dh) % 2))
        greet(((ylo + i // 8) % 2, (x + (i // 2) % 4) % NX, (core + i % 2) % 2, z, yhi))

    loads[0].wait()
    pl.semaphore_wait(barrier, 32 - own_source.astype(jnp.int32))

    def scatter(h):
        return pltpu.make_async_remote_copy(
            src_ref=colp.at[row], dst_ref=rowp.at[row], send_sem=row_send.at[h], recv_sem=row_recv.at[row],
            device_id=(z // NX, z % NX, yhi, plane, h), device_id_type=MESH,
        )

    for h in range(2):
        mine = jnp.logical_and(own_source, yhi == h)

        @pl.when(jnp.logical_not(mine))
        def _():
            scatter(h).start()

        @pl.when(mine)
        def _():
            pltpu.make_async_copy(pair_hbm, rowp.at[row], row_recv.at[row]).start()

    def to_partner(slot, sem):
        return pltpu.make_async_remote_copy(
            src_ref=colp.at[slot], dst_ref=colp.at[slot], send_sem=col_send.at[sem], recv_sem=col_recv.at[slot],
            device_id=(ylo, x, 1 - core, z, yhi), device_id_type=MESH,
        )

    to_partner(row, 7).start()
    own_sends = []
    for i, (dy, dx) in enumerate(PEERS):
        send = pltpu.make_async_remote_copy(
            src_ref=colp.at[row], dst_ref=colp.at[row], send_sem=col_send.at[i], recv_sem=col_recv.at[row],
            device_id=((ylo + dy) % 2, (x + dx) % NX, core, z, yhi), device_id_type=MESH,
        )
        send.start()
        own_sends.append(send)

    loads[1].wait()
    loads[2].wait()
    diagonal = row * stat.shape[0] - col * stat.shape[1]
    acc[...] = jnp.zeros_like(acc)

    @pl.loop(0, stat.shape[0] // SLICE)
    def _(i):
        start = pl.multiple_of(i * SLICE, SLICE)
        rows = pl.ds(start, SLICE)
        shape = (SLICE, stat.shape[1])
        ahead = lax.broadcasted_iota(jnp.int32, shape, 1) - lax.broadcasted_iota(jnp.int32, shape, 0)
        one = jnp.where(ahead == diagonal + start, 1.0, 0.0).astype(jnp.float32)
        s = stat[rows, :] - one
        g = imag[rows, :] - one
        d = s - g
        pole = jnp.sqrt((g * g + 0.25) / (d * d + 0.25))
        top = -s * pole
        for e in range(NE):
            kmat[e, rows, :] = (top / (pole + freq[e])).astype(jnp.bfloat16)

    def row_slot(slot):
        return pltpu.make_async_copy(rowp.at[slot], rowp.at[slot], row_recv.at[slot])

    def col_slot(slot):
        return pltpu.make_async_copy(colp.at[slot], colp.at[slot], col_recv.at[slot])

    def ring(slot, sem, step):
        return pltpu.make_async_remote_copy(
            src_ref=rowp.at[slot], dst_ref=rowp.at[slot], send_sem=row_send.at[sem], recv_sem=row_recv.at[slot],
            device_id=(ylo, x, core, (z + NZ + step) % NZ, yhi), device_id_type=MESH,
        )

    def up_slot(i):
        return 2 * ((z + NZ - i // 2) % NZ) + i % 2

    def down_slot(i):
        return 2 * ((z + i // 2) % NZ) + 1 - i % 2

    def piece_of(j):
        return (z + NZ + ((j + 1) // 2) * (2 * (j % 2) - 1)) % NZ

    def compute(piece):
        left = rowp[pl.ds(2 * piece, 2)].reshape(256, rowp.shape[2])

        @pl.loop(0, NE)
        def _(e):
            projected = jnp.dot(left, kmat[e], preferred_element_type=jnp.float32)
            terms = projected * colp[pl.ds(2 * piece, 2)].reshape(256, colp.shape[2]).astype(jnp.float32)
            lanes = terms[:, 0:128]
            for g in range(1, 6):
                lanes = lanes + terms[:, g * 128:(g + 1) * 128]
            total = acc[e, 0:64, :]
            for b in range(4):
                offset = freq[e] - band[4 * piece + b]
                weight = 1.0 / (1.0 + jnp.full((1, 128), offset * offset, jnp.float32))
                total = total + weight * lanes[b * 64:(b + 1) * 64, :]
            acc[e, 0:64, :] = total

    for i in range(7):
        if i != 1:
            row_slot(up_slot(i)).wait()
            row_slot(down_slot(i)).wait()
        ring(up_slot(i), 2 + 2 * i, 1).start()
        ring(down_slot(i), 3 + 2 * i, -1).start()
        for p in (2 * i, 2 * i + 1):
            if p < len(PEERS):
                dy, dx = PEERS[p]
                slot = 2 * (4 * ((ylo + NZ - dy) % 2) + (x + NX - dx) % NX) + core
                col_slot(slot).wait()
                to_partner(slot, 8 + p).start()
        if i == 4:
            for q in range(8):
                col_slot(2 * q + 1 - core).wait()

            @pl.loop(0, 3)
            def _(j):
                compute(piece_of(j))
        if i == 6:
            @pl.loop(3, 5)
            def _(j):
                compute(piece_of(j))

    row_slot(up_slot(7)).wait()
    row_slot(down_slot(7)).wait()

    @pl.loop(5, 7)
    def _(j):
        compute(piece_of(j))

    far = (z + 4) % NZ
    row_slot(2 * far).wait()
    row_slot(2 * far + 1).wait()
    compute(far)

    ones = jnp.ones((8, 128), jnp.float32)
    which = lax.broadcasted_iota(jnp.int32, (8, 128), 0)
    tile = jnp.zeros((8, 128), jnp.float32)
    for e in range(NE):
        summed = lax.dot_general(
            ones, acc[e], (((1,), (1,)), ((), ())),
            precision=lax.Precision.HIGHEST, preferred_element_type=jnp.float32,
        )
        tile = tile + jnp.where(which == e, summed, 0.0)

    def exchange(buffer, me, value, target, recv, send):
        buffer[me] = value

        def copy(i, device):
            return pltpu.make_async_remote_copy(
                src_ref=buffer.at[me], dst_ref=buffer.at[me], send_sem=send.at[i], recv_sem=recv.at[me],
                device_id=device, device_id_type=MESH,
            )

        @pl.loop(1, 16)
        def _(i):
            copy(i, target(i)).start()

        @pl.loop(1, 16)
        def _(i):
            slot = (me + i) % 16
            pltpu.make_async_copy(buffer.at[slot], buffer.at[slot], recv.at[slot]).wait()

        @pl.loop(1, 16)
        def _(i):
            copy(i, target(i)).wait_send()

        total = buffer[0]
        for i in range(1, 16):
            total = total + buffer[i]
        return total

    tile = exchange(red1, col, tile, lambda i: (ylo, x, core, (z + i // 2) % NZ, (yhi + i % 2) % 2), r1_recv, r1_send)
    out[...] = exchange(
        red2, row, tile,
        lambda i: ((ylo + i // 8) % 2, (x + (i // 2) % 4) % NX, (core + i % 2) % 2, z, yhi), r2_recv, r2_send,
    )

    for h in range(2):
        @pl.when(jnp.logical_not(jnp.logical_and(own_source, yhi == h)))
        def _():
            scatter(h).wait_send()
    for send in own_sends:
        send.wait_send()
    to_partner(row, 7).wait_send()
    for p, (dy, dx) in enumerate(PEERS):
        slot = 2 * (4 * ((ylo + NZ - dy) % 2) + (x + NX - dx) % NX) + core
        to_partner(slot, 8 + p).wait_send()
    for i in range(7):
        ring(up_slot(i), 2 + 2 * i, 1).wait_send()
        ring(down_slot(i), 3 + 2 * i, -1).wait_send()


def shards(eps_static, eps_imag, frequency_grid, band_energy, pair_elements):
    height, breadth = eps_static.shape
    rows = pair_elements.shape[0] * pair_elements.shape[1]
    pair = pair_elements.reshape(rows, breadth)
    anywhere = pl.BlockSpec(memory_space=pl.ANY)
    scalars = pl.BlockSpec(memory_space=pltpu.SMEM)
    dma = pltpu.SemaphoreType.DMA
    summed = pl.pallas_call(
        kernel,
        out_shape=jax.ShapeDtypeStruct((8, 128), jnp.float32),
        in_specs=[anywhere, anywhere, scalars, scalars, anywhere],
        out_specs=pl.BlockSpec(memory_space=pltpu.VMEM),
        scratch_shapes=[
            pltpu.VMEM((16, rows, height), jnp.bfloat16),
            pltpu.VMEM((16, rows, breadth), jnp.bfloat16),
            pltpu.VMEM((NE, height, breadth), jnp.bfloat16),
            pltpu.VMEM((height, breadth), jnp.float32),
            pltpu.VMEM((height, breadth), jnp.float32),
            pltpu.VMEM((NE, 128, 128), jnp.float32),
            pltpu.VMEM((16, 8, 128), jnp.float32),
            pltpu.VMEM((16, 8, 128), jnp.float32),
            dma((3,)), dma((16,)), dma((16,)), dma((16,)), dma((15,)),
            dma((16,)), dma((16,)), dma((16,)), dma((16,)),
        ],
        compiler_params=pltpu.CompilerParams(
            collective_id=0, has_side_effects=True, vmem_limit_bytes=60 * 1024 * 1024
        ),
    )(eps_static, eps_imag, frequency_grid, band_energy, pair)
    states = pair_elements.shape[1] // lax.axis_size(GCOL)
    return lax.dynamic_slice(summed, (0, lax.axis_index(GCOL) * states), (NE, states))


def solution(mesh):
    finer = Mesh(
        mesh.devices.reshape(2, 4, 2, 8, 2), ("grow_0", "grow_1", "grow_2", "gcol_0", "gcol_1")
    )
    in_specs = (P(GROW, GCOL), P(GROW, GCOL), P(), P(), P(GROW, None, GCOL))
    out_specs = P(None, GCOL)
    return jax.shard_map(
        shards, mesh=finer, in_specs=in_specs, out_specs=out_specs, check_vma=False
    )
```

time: 211 us -> 102 us (0.48)
  Pallas kernels: 0 us -> 101 us
  waiting for transfers between devices: 101 us -> 0 us
  blocking collectives: 45.1 us -> 0 us
  matrix products: 27.1 us -> 0 us
  between operations: 13.5 us -> 0.01 us
  local copies, waits for them, and re-layouts: 13.8 us -> 1.34 us
  other arithmetic: 5.74 us -> 0 us
  starting transfers between devices: 5.07 us -> 0 us
    pallas_call x0 -> x1, Pallas kernels: none -> 101 us  [shards(): pl.pallas_call(kernel, out_shape=jax.ShapeDtypeStruct((8, 128), jnp.float...]
    all_gather x2 -> x0, waiting for transfers between devices: 99.9 us -> none  [the longest x1 53.7 us: shards(): column_panel = lax.all_gather(pair_elements, GROW, axis=0, tiled=True)]
    all_to_all x3 -> x0, blocking collectives: 34.6 us -> none  [the longest x1 17.6 us: summed_on_arrival(): lax.all_to_all(split_up(shard, dim, devices), axis, 0, 0, tiled=True)]
    dot_general x4 -> x0, matrix products: 27.1 us -> none  [the longest x3 27 us: shards(): projected = jnp.dot(left_rows, kernel, preferred_element_type=jnp.float32)]
    all_gather x1 -> x0, blocking collectives: 10.5 us -> none  [gathered_by_axis(): shard = lax.all_gather(shard, axis, axis=dim, tiled=True)]
    convert_element_type x1 -> x0, local copies, waits for them, and re-layouts: 6.6 us -> none  [shards(): terms.append(jnp.sum(projected * right_rows, axis=1))]
    convert_element_type x1 -> x0, other arithmetic: 5.03 us -> none  [shards(): terms.append(jnp.sum(projected * right_rows, axis=1))]
    all_to_all x1 -> x0, starting transfers between devices: 5.03 us -> none  [turned_blocks(): out = lax.all_to_all(out, axes[k], k, k, tiled=True)]
  transfers between devices with their start and end apart: 3 -> 0, of which waited for: 2 -> 0; matrix products, arithmetic and copies ran while one was open for 9% -> 0% of each run, Pallas kernels for 0% -> 0%
where the time goes in v1:
time: 102 us
  Pallas kernels  101 us (99%)
  local copies, waits for them, and re-layouts  1.34 us (1%)
    pallas_call x1, Pallas kernels, shards(): pl.pallas_call(kernel, out_shape=jax.ShapeDtypeStruct((8, 128), jnp.float...  101 us

profile of v1, /device:TPU:1, one launch (start us, length us, event | category | flops | bytes accessed | tf_op | source)
XLA Modules:
  0.0 102.4 jit_solution(16319551818867716458)
XLA Ops:
  0.0 101.0 %shard_map.55 = f32[8,128]{1,0:T(8,128)} custom-call(f32[768,768]{1,0:T(8,128)} %static_hbm.1, f32[768,768]{1,0:T(8,128)} %imag_hbm.1, f32[3]{0:T(128)} %freq.1, f32[32]{0:T(128)} %band.1, bf16[128,768]{1,0:T(8,128)(2,1)} %bitcast.1), custom_call_target="tpu_custom_call" | custom-call | tf_op jit(solution)/shard_map/pallas_call | solution.py:250
  101.0 1.3 %constant_dynamic-slice_fusion = f32[3,4]{1,0:T(4,128)} fusion(f32[8,128]{1,0:T(8,128)} %shard_map.55, s32[]{:T(128)S(6)} %select_n.3), kind=kLoop, calls=%fused_computation | loop fusion | bytes 100 | tf_op jit(solution)/shard_map/dynamic_slice | solution.py:272

commit v2 on v1

v2 whole, which is shorter than its diff:
```python
import jax
import jax.numpy as jnp
from jax import lax
from jax.experimental import pallas as pl
from jax.experimental.pallas import tpu as pltpu
from jax.sharding import Mesh
from jax.sharding import PartitionSpec as P

NE = 3
NX = 4
NZ = 8
GROW = ("grow_0", "grow_1", "grow_2")
GCOL = ("gcol_0", "gcol_1")
MESH = pl.DeviceIdType.MESH
SLICE = 16
ACROSS = (0, 2, -2, 4)
EVERY = (0, 1, -1, 2, -2, 3, -3, 4)


def kernel(
    static_hbm, imag_hbm, freq, band, pair_hbm, out,
    rowp, colp, kmat, stat, imag, acc, red1, red2,
    in_sem, sent, row_recv, col_recv, r1_recv, r1_send, r2_recv, r2_send,
):
    ylo, x, core = (lax.axis_index(a) for a in GROW)
    z, yhi = (lax.axis_index(a) for a in GCOL)
    plane = NX * ylo + x
    row = plane * 2 + core
    col = z * 2 + yhi
    half = rowp.shape[1] // 2
    partner = (ylo, x, 1 - core, z, yhi)

    def in_plane(i):
        return ((ylo + (i // 4) % 2) % 2, (x + i % 4) % NX, core, z, (yhi + i // 8) % 2)

    def along_z(i):
        return (ylo, x, (core + i % 2) % 2, (z + i // 2) % NZ, yhi)

    loads = [
        pltpu.make_async_copy(pair_hbm, colp.at[row], in_sem.at[0]),
        pltpu.make_async_copy(static_hbm, stat, in_sem.at[1]),
        pltpu.make_async_copy(imag_hbm, imag, in_sem.at[2]),
    ]
    for load in loads:
        load.start()

    barrier = pltpu.get_barrier_semaphore()

    def greet(device):
        pl.semaphore_signal(barrier, inc=1, device_id=device, device_id_type=MESH)

    stays = jnp.logical_and(jnp.logical_and(plane == z, z == 0), core == yhi)
    origin = (z + plane) % NZ

    @pl.when(jnp.logical_not(stays))
    def _():
        greet((origin // NX, origin % NX, yhi, plane, core))

    @pl.loop(1, 16)
    def _(i):
        greet(in_plane(i))
        greet(along_z(i))

    loads[1].wait()
    loads[2].wait()
    diagonal = row * stat.shape[0] - col * stat.shape[1]
    acc[...] = jnp.zeros_like(acc)

    @pl.loop(0, stat.shape[0] // SLICE)
    def _(i):
        start = pl.multiple_of(i * SLICE, SLICE)
        rows = pl.ds(start, SLICE)
        shape = (SLICE, stat.shape[1])
        ahead = lax.broadcasted_iota(jnp.int32, shape, 1) - lax.broadcasted_iota(jnp.int32, shape, 0)
        one = jnp.where(ahead == diagonal + start, 1.0, 0.0).astype(jnp.float32)
        s = stat[rows, :] - one
        g = imag[rows, :] - one
        d = s - g
        pole = jnp.sqrt((g * g + 0.25) / (d * d + 0.25))
        top = -s * pole
        for e in range(NE):
            kmat[e, rows, :] = (top / (pole + freq[e])).astype(jnp.bfloat16)

    loads[0].wait()
    pl.semaphore_wait(barrier, 31 - stays.astype(jnp.int32))

    started = []

    def send(src, dst, recv, device):
        copy = pltpu.make_async_remote_copy(
            src_ref=src, dst_ref=dst, send_sem=sent.at[len(started)], recv_sem=recv,
            device_id=device, device_id_type=MESH,
        )
        started.append(copy)
        return copy

    first = send(colp.at[row], rowp.at[row], row_recv.at[2 * row], (z // NX, z % NX, yhi, (plane + NZ - z) % NZ, core))

    @pl.when(jnp.logical_not(stays))
    def _():
        first.start()

    @pl.when(stays)
    def _():
        pltpu.make_async_copy(pair_hbm, rowp.at[row], row_recv.at[2 * row]).start()

    def block(chain, far):
        return 2 * ((z + plane + 2 * NZ - far) % NZ) + (yhi + chain) % 2

    arrived = set()

    def need(chain, far, part):
        whole = far == 0 or (chain == 1 and far in ACROSS)
        key = (chain, far) if whole else (chain, far, part)
        if key in arrived:
            return
        arrived.add(key)
        b = block(chain, far)
        if whole:
            ref, sem = rowp.at[b], row_recv.at[2 * b]
        else:
            ref, sem = rowp.at[b, pl.ds(part * half, half)], row_recv.at[2 * b + part]
        pltpu.make_async_copy(ref, ref, sem).wait()

    def along(chain, far, parts=((0, 1), (0, 1))):
        for step, side in ((1, parts[0]), (-1, parts[1])):
            for part in side:
                need(chain, step * far, part)
                b = block(chain, step * far)
                ref = rowp.at[b, pl.ds(part * half, half)]
                send(ref, ref, row_recv.at[2 * b + part], (ylo, x, core, (z + NZ + step) % NZ, yhi)).start()

    def across(far):
        need(0, far, 0)
        need(0, far, 1)
        b = block(0, far)
        send(rowp.at[b], rowp.at[b], row_recv.at[2 * b], (ylo, x, core, z, 1 - yhi)).start()

    def col_slot(a, b, c):
        return 2 * (NX * a + b) + c

    def col_wait(slot):
        pltpu.make_async_copy(colp.at[slot], colp.at[slot], col_recv.at[slot]).wait()

    def col_send(slot, device):
        send(colp.at[slot], colp.at[slot], col_recv.at[slot], device).start()

    def relay(i):
        slot = col_slot((ylo + i // 3) % 2, (x + NX - (1, 3, 2)[i % 3]) % NX, core)
        col_wait(slot)
        col_send(slot, partner)

    def compute(b0, b1):
        left = jnp.concatenate([rowp[b0], rowp[b1]], axis=0)
        rows = rowp.shape[1]

        @pl.loop(0, NE)
        def _(e):
            projected = jnp.dot(left, kmat[e], preferred_element_type=jnp.float32)
            total = acc[e, 0:half, :]
            for n, b in enumerate((b0, b1)):
                terms = projected[n * rows:(n + 1) * rows] * colp[b].astype(jnp.float32)
                lanes = terms[:, 0:128]
                for g in range(1, terms.shape[1] // 128):
                    lanes = lanes + terms[:, g * 128:(g + 1) * 128]
                for part in range(2):
                    offset = freq[e] - band[2 * b + part]
                    weight = 1.0 / (1.0 + jnp.full((1, 128), offset * offset, jnp.float32))
                    total = total + weight * lanes[part * half:(part + 1) * half, :]
            acc[e, 0:half, :] = total

    def compute_pair(chain, far):
        for f in (far, -far):
            need(chain, f, 0)
            need(chain, f, 1)
        compute(block(chain, far), block(chain, -far))

    def compute_both(far):
        for chain in range(2):
            need(chain, far, 0)
            need(chain, far, 1)
        compute(block(0, far), block(1, far))

    col_send(row, (1 - ylo, x, core, z, yhi))
    col_send(row, partner)
    for dx in (1, 3, 2):
        col_send(row, (ylo, (x + dx) % NX, core, z, yhi))

    along(0, 0)
    across(0)
    along(0, 1)
    neighbour = col_slot(1 - ylo, x, core)
    col_wait(neighbour)
    for dx in (1, 3, 2):
        col_send(neighbour, (ylo, (x + dx) % NX, core, z, yhi))
    col_send(neighbour, partner)
    relay(0)
    along(0, 2)
    relay(1)
    across(2)
    across(-2)
    along(0, 3, ((0,), (1,)))
    along(1, 0)
    for i in range(2, 6):
        relay(i)
    for a in range(2):
        for b in range(NX):
            col_wait(col_slot(a, b, 1 - core))
    compute_both(0)
    across(4)
    compute_pair(0, 1)
    compute_pair(0, 2)
    along(1, 2)
    compute_pair(0, 3)
    compute_pair(1, 2)
    compute_pair(1, 1)
    compute_both(4)
    compute_pair(1, 3)

    ones = jnp.ones((8, 128), jnp.float32)
    which = lax.broadcasted_iota(jnp.int32, (8, 128), 0)
    tile = jnp.zeros((8, 128), jnp.float32)
    for e in range(NE):
        summed = lax.dot_general(
            ones, acc[e], (((1,), (1,)), ((), ())),
            precision=lax.Precision.HIGHEST, preferred_element_type=jnp.float32,
        )
        tile = tile + jnp.where(which == e, summed, 0.0)

    def exchange(buffer, me, value, target, recv, sem):
        buffer[me] = value

        def copy(i):
            return pltpu.make_async_remote_copy(
                src_ref=buffer.at[me], dst_ref=buffer.at[me], send_sem=sem.at[i], recv_sem=recv.at[me],
                device_id=target(i), device_id_type=MESH,
            )

        @pl.loop(1, 16)
        def _(i):
            copy(i).start()

        @pl.loop(1, 16)
        def _(i):
            slot = (me + i) % 16
            pltpu.make_async_copy(buffer.at[slot], buffer.at[slot], recv.at[slot]).wait()

        @pl.loop(1, 16)
        def _(i):
            copy(i).wait_send()

        total = buffer[0]
        for i in range(1, 16):
            total = total + buffer[i]
        return total

    tile = exchange(red1, NX * (2 * yhi + ylo) + x, tile, in_plane, r1_recv, r1_send)
    out[...] = exchange(red2, 2 * z + core, tile, along_z, r2_recv, r2_send)

    @pl.when(jnp.logical_not(stays))
    def _():
        first.wait_send()

    for copy in started[1:]:
        copy.wait_send()


def shards(eps_static, eps_imag, frequency_grid, band_energy, pair_elements):
    height, breadth = eps_static.shape
    rows = pair_elements.shape[0] * pair_elements.shape[1]
    pair = pair_elements.reshape(rows, breadth)
    anywhere = pl.BlockSpec(memory_space=pl.ANY)
    scalars = pl.BlockSpec(memory_space=pltpu.SMEM)
    dma = pltpu.SemaphoreType.DMA
    summed = pl.pallas_call(
        kernel,
        out_shape=jax.ShapeDtypeStruct((8, 128), jnp.float32),
        in_specs=[anywhere, anywhere, scalars, scalars, anywhere],
        out_specs=pl.BlockSpec(memory_space=pltpu.VMEM),
        scratch_shapes=[
            pltpu.VMEM((16, rows, height), jnp.bfloat16),
            pltpu.VMEM((16, rows, breadth), jnp.bfloat16),
            pltpu.VMEM((NE, height, breadth), jnp.bfloat16),
            pltpu.VMEM((height, breadth), jnp.float32),
            pltpu.VMEM((height, breadth), jnp.float32),
            pltpu.VMEM((NE, 128, 128), jnp.float32),
            pltpu.VMEM((16, 8, 128), jnp.float32),
            pltpu.VMEM((16, 8, 128), jnp.float32),
            dma((3,)), dma((48,)), dma((32,)), dma((16,)),
            dma((16,)), dma((16,)), dma((16,)), dma((16,)),
        ],
        compiler_params=pltpu.CompilerParams(
            collective_id=0, has_side_effects=True, vmem_limit_bytes=60 * 1024 * 1024
        ),
    )(eps_static, eps_imag, frequency_grid, band_energy, pair)
    states = pair_elements.shape[1] // lax.axis_size(GCOL)
    return lax.dynamic_slice(summed, (0, lax.axis_index(GCOL) * states), (NE, states))


def solution(mesh):
    finer = Mesh(
        mesh.devices.reshape(2, 4, 2, 8, 2), ("grow_0", "grow_1", "grow_2", "gcol_0", "gcol_1")
    )
    in_specs = (P(GROW, GCOL), P(GROW, GCOL), P(), P(), P(GROW, None, GCOL))
    out_specs = P(None, GCOL)
    return jax.shard_map(
        shards, mesh=finer, in_specs=in_specs, out_specs=out_specs, check_vma=False
    )
```

time: 102 us -> 74 us (0.73)
  Pallas kernels: 101 us -> 72.5 us
    pallas_call x1, Pallas kernels: 101 us -> 72.5 us  [shards(): pl.pallas_call(kernel, out_shape=jax.ShapeDtypeStruct((8, 128), jnp.float...]
where the time goes in v2:
time: 74 us; the launch traced here: 73.9 us
  Pallas kernels  72.5 us (98%)
  local copies, waits for them, and re-layouts  1.34 us (2%)
    pallas_call x1, Pallas kernels, shards(): pl.pallas_call(kernel, out_shape=jax.ShapeDtypeStruct((8, 128), jnp.float...  72.5 us

profile of v2, /device:TPU:1, one launch (start us, length us, event | category | flops | bytes accessed | tf_op | source)
XLA Modules:
  0.0 73.9 jit_solution(11336600588038883391)
XLA Ops:
  0.0 72.5 %shard_map.55 = f32[8,128]{1,0:T(8,128)} custom-call(f32[768,768]{1,0:T(8,128)} %static_hbm.1, f32[768,768]{1,0:T(8,128)} %imag_hbm.1, f32[3]{0:T(128)} %freq.1, f32[32]{0:T(128)} %band.1, bf16[128,768]{1,0:T(8,128)(2,1)} %bitcast.1), custom_call_target="tpu_custom_call" | custom-call | tf_op jit(solution)/shard_map/pallas_call | solution.py:275
  72.5 1.3 %constant_dynamic-slice_fusion = f32[3,4]{1,0:T(4,128)} fusion(f32[8,128]{1,0:T(8,128)} %shard_map.55, s32[]{:T(128)S(6)} %select_n.3), kind=kLoop, calls=%fused_computation | loop fusion | bytes 100 | tf_op jit(solution)/shard_map/dynamic_slice | solution.py:297

commit v3 on v2

v3 whole, which is shorter than its diff:
```python
import jax
import jax.numpy as jnp
from jax import lax
from jax.experimental import pallas as pl
from jax.experimental.pallas import tpu as pltpu
from jax.sharding import Mesh
from jax.sharding import PartitionSpec as P

NE = 3
NX = 4
NZ = 8
GROW = ("grow_0", "grow_1", "grow_2")
GCOL = ("gcol_0", "gcol_1")
MESH = pl.DeviceIdType.MESH
SLICE = 16
EVERY = (0, 1, -1, 2, -2, 3, -3, 4)
PROGRAM = (
    ("n",),
    ("z", 0, 0, 0), ("y", 0, 0),
    ("r", 0), ("r", 1),
    ("z", 0, 0, 1), ("y", 0, 1), ("z", 0, 1, 0), ("y", 1, 0),
    ("r", 2),
    ("y", -1, 0), ("z", 0, 1, 1), ("y", 1, 1),
    ("d", (0, 0), (1, 0)),
    ("z", 0, 2, 0),
    ("r", 3),
    ("y", -1, 1), ("z", 0, 2, 1),
    ("d", (0, 1), (0, -1)),
    ("z", 1, 1, 0), ("r", 4), ("y", 3, 1), ("z", 0, 3, 0), ("z", 0, 3, 1),
    ("d", (0, 2), (0, -2)),
    ("y", -3, 1), ("z", 1, 1, 1),
    ("r", 5), ("y", 4, 0), ("z", 1, 2, 0),
    ("w",),
    ("c", (1, 1), (1, -1)),
    ("z", 1, 3, 1),
    ("c", (0, 3), (0, -3)),
    ("m", (0, 0), (1, 0), (0, 1), (0, -1), (0, 2), (0, -2)),
    ("c", (0, 4),), ("c", (1, 2), (1, -2)), ("c", (1, 3), (1, -3)), ("c", (1, 4),),
)


def kernel(
    static_hbm, imag_hbm, freq, band, pair_hbm, out,
    rowp, colp, kmat, stat, imag, ahead, acc, red1, red2,
    in_sem, sent, row_recv, col_recv, r1_recv, r1_send, r2_recv, r2_send,
):
    ylo, x, core = (lax.axis_index(a) for a in GROW)
    z, yhi = (lax.axis_index(a) for a in GCOL)
    plane = NX * ylo + x
    row = plane * 2 + core
    col = z * 2 + yhi
    half = rowp.shape[1] // 2
    partner = (ylo, x, 1 - core, z, yhi)
    xs = [lax.rem(x + i, NX) for i in range(NX)]
    zs = [lax.rem(z + i, NZ) for i in range(NZ)]
    cores, ylos, yhis = (core, 1 - core), (ylo, 1 - ylo), (yhi, 1 - yhi)
    in_plane = [
        (ylos[a], xs[b], core, z, yhis[c]) for c in (1, 0) for b in (2, 1, 3, 0) for a in (1, 0) if (a, b, c) != (0, 0, 0)
    ]
    along_z = [
        (ylo, x, cores[a], zs[b], yhi) for b in (4, 3, 5, 2, 6, 1, 7, 0) for a in (1, 0) if (a, b) != (0, 0)
    ]

    loads = [
        pltpu.make_async_copy(pair_hbm, colp.at[row], in_sem.at[0]),
        pltpu.make_async_copy(static_hbm, stat, in_sem.at[1]),
        pltpu.make_async_copy(imag_hbm, imag, in_sem.at[2]),
    ]
    for load in loads:
        load.start()

    barrier = pltpu.get_barrier_semaphore()

    def greet(device):
        pl.semaphore_signal(barrier, inc=1, device_id=device, device_id_type=MESH)

    stays = jnp.logical_and(jnp.logical_and(plane == z, z == 0), core == yhi)
    origin = lax.rem(z + plane, NZ)

    @pl.when(jnp.logical_not(stays))
    def _():
        greet((origin // NX, lax.rem(origin, NX), yhi, plane, core))

    for device in along_z + in_plane:
        greet(device)

    loads[0].wait()
    pl.semaphore_wait(barrier, 31 - stays.astype(jnp.int32))

    started = []

    def send(src, dst, recv, device):
        copy = pltpu.make_async_remote_copy(
            src_ref=src, dst_ref=dst, send_sem=sent.at[len(started)], recv_sem=recv,
            device_id=device, device_id_type=MESH,
        )
        started.append(copy)
        return copy

    place = (z // NX, lax.rem(z, NX), yhi, lax.rem(plane + NZ - z, NZ), core)

    def piece(panel, slot, part):
        return panel.at[slot, pl.ds(part * half, half)]

    first = [send(piece(colp, row, t), piece(rowp, row, t), row_recv.at[2 * row + t], place) for t in range(2)]

    @pl.when(jnp.logical_not(stays))
    def _():
        for copy in first:
            copy.start()

    @pl.when(stays)
    def _():
        for t in range(2):
            pltpu.make_async_copy(pair_hbm.at[pl.ds(t * half, half)], piece(rowp, row, t), row_recv.at[2 * row + t]).start()

    pieces = {far: 2 * lax.rem(z + plane + 2 * NZ - far, NZ) for far in EVERY}
    pieces[-4] = pieces[4]

    def block(chain, far):
        return pieces[far] + yhis[chain]

    arrived = set()

    def need(chain, far, part):
        far = 4 if far == -4 else far
        if (chain, far, part) not in arrived:
            arrived.add((chain, far, part))
            b = block(chain, far)
            pltpu.make_async_copy(piece(rowp, b, part), piece(rowp, b, part), row_recv.at[2 * b + part]).wait()

    def pass_on(chain, far, part, device):
        need(chain, far, part)
        b = block(chain, far)
        send(piece(rowp, b, part), piece(rowp, b, part), row_recv.at[2 * b + part], device).start()

    def along(chain, far, part):
        for way in (1, -1) if far < 3 else ((1,) if part == 0 else (-1,)):
            pass_on(chain, way * far, part, (ylo, x, core, zs[way % NZ], yhi))

    def across(far, part):
        pass_on(0, far, part, (ylo, x, core, z, yhis[1]))

    def col_slot(a, b, c):
        return 2 * (NX * a + b) + c

    def col_wait(slot):
        pltpu.make_async_copy(colp.at[slot], colp.at[slot], col_recv.at[slot]).wait()

    def col_send(slot, device):
        send(colp.at[slot], colp.at[slot], col_recv.at[slot], device).start()

    def relay(i):
        slot = col_slot(ylos[i // 3], xs[(3, 1, 2)[i % 3]], core)
        col_wait(slot)
        col_send(slot, partner)

    def project(blocks, e):
        left = jnp.concatenate([rowp[b] for b in blocks], axis=0)
        return jnp.dot(left, kmat[e], preferred_element_type=jnp.float32)

    def weighted(projected, b, e):
        terms = projected * colp[b].astype(jnp.float32)
        lanes = terms[:, 0:128]
        for g in range(1, terms.shape[1] // 128):
            lanes = lanes + terms[:, g * 128:(g + 1) * 128]
        total = 0.0
        for part in range(2):
            offset = freq[e] - band[2 * b + part]
            weight = 1.0 / (1.0 + jnp.full((1, 128), offset * offset, jnp.float32))
            total = total + weight * lanes[part * half:(part + 1) * half, :]
        return total

    kept = {}

    def rows_of(n):
        return slice(n * rowp.shape[1], (n + 1) * rowp.shape[1])

    def project_ahead(keys):
        blocks = [block(*key) for key in keys]
        for e in range(NE):
            projected = project(blocks, e)
            for n, key in enumerate(keys):
                ahead[kept.setdefault(key, len(kept)), e] = projected[rows_of(n)]

    def finish(keys):
        for e in range(NE):
            total = acc[e, 0:half, :]
            for key in keys:
                total = total + weighted(ahead[kept[key], e], block(*key), e)
            acc[e, 0:half, :] = total

    def compute(keys):
        blocks = [block(*key) for key in keys]
        for e in range(NE):
            projected = project(blocks, e)
            total = acc[e, 0:half, :]
            for n, b in enumerate(blocks):
                total = total + weighted(projected[rows_of(n)], b, e)
            acc[e, 0:half, :] = total

    col_send(row, (ylos[1], x, core, z, yhi))
    col_send(row, partner)
    for dx in (1, 3, 2):
        col_send(row, (ylo, xs[dx], core, z, yhi))

    loads[1].wait()
    loads[2].wait()
    diagonal = row * stat.shape[0] - col * stat.shape[1]
    acc[...] = jnp.zeros_like(acc)

    @pl.loop(0, stat.shape[0] // SLICE)
    def _(i):
        start = pl.multiple_of(i * SLICE, SLICE)
        rows = pl.ds(start, SLICE)
        shape = (SLICE, stat.shape[1])
        ahead = lax.broadcasted_iota(jnp.int32, shape, 1) - lax.broadcasted_iota(jnp.int32, shape, 0)
        one = jnp.where(ahead == diagonal + start, 1.0, 0.0).astype(jnp.float32)
        s = stat[rows, :] - one
        g = imag[rows, :] - one
        d = s - g
        pole = jnp.sqrt((g * g + 0.25) / (d * d + 0.25))
        top = -s * pole
        for e in range(NE):
            kmat[e, rows, :] = (top / (pole + freq[e])).astype(jnp.bfloat16)

    for op, *args in PROGRAM:
        if op == "z":
            along(*args)
        elif op == "y":
            across(*args)
        elif op == "n":
            neighbour = col_slot(ylos[1], x, core)
            col_wait(neighbour)
            for dx in (1, 3, 2):
                col_send(neighbour, (ylo, xs[dx], core, z, yhi))
            col_send(neighbour, partner)
        elif op == "r":
            relay(*args)
        elif op == "w":
            for a in range(2):
                for b in range(NX):
                    col_wait(col_slot(a, b, 1 - core))
        else:
            for chain, far in args:
                need(chain, far, 0)
                need(chain, far, 1)
            {"d": project_ahead, "m": finish, "c": compute}[op](args)

    ones = jnp.ones((8, 128), jnp.float32)
    which = lax.broadcasted_iota(jnp.int32, (8, 128), 0)
    tile = jnp.zeros((8, 128), jnp.float32)
    for e in range(NE):
        summed = lax.dot_general(
            ones, acc[e], (((1,), (1,)), ((), ())),
            precision=lax.Precision.HIGHEST, preferred_element_type=jnp.float32,
        )
        tile = tile + jnp.where(which == e, summed, 0.0)

    def exchange(buffer, me, value, devices, recv, sem):
        buffer[me] = value
        copies = [
            pltpu.make_async_remote_copy(
                src_ref=buffer.at[me], dst_ref=buffer.at[me], send_sem=sem.at[i], recv_sem=recv.at[me],
                device_id=device, device_id_type=MESH,
            )
            for i, device in enumerate(devices)
        ]
        for copy in copies:
            copy.start()
        for i in range(1, 16):
            slot = lax.rem(me + i, 16)
            pltpu.make_async_copy(buffer.at[slot], buffer.at[slot], recv.at[slot]).wait()
        total = buffer[0]
        for i in range(1, 16):
            total = total + buffer[i]
        return total, copies

    tile, last = exchange(red1, NX * (2 * yhi + ylo) + x, tile, in_plane, r1_recv, r1_send)
    out[...], more = exchange(red2, 2 * z + core, tile, along_z, r2_recv, r2_send)

    @pl.when(jnp.logical_not(stays))
    def _():
        for copy in first:
            copy.wait_send()

    for copy in started[2:] + last + more:
        copy.wait_send()


def shards(eps_static, eps_imag, frequency_grid, band_energy, pair_elements):
    height, breadth = eps_static.shape
    rows = pair_elements.shape[0] * pair_elements.shape[1]
    pair = pair_elements.reshape(rows, breadth)
    anywhere = pl.BlockSpec(memory_space=pl.ANY)
    scalars = pl.BlockSpec(memory_space=pltpu.SMEM)
    dma = pltpu.SemaphoreType.DMA
    summed = pl.pallas_call(
        kernel,
        out_shape=jax.ShapeDtypeStruct((8, 128), jnp.float32),
        in_specs=[anywhere, anywhere, scalars, scalars, anywhere],
        out_specs=pl.BlockSpec(memory_space=pltpu.VMEM),
        scratch_shapes=[
            pltpu.VMEM((16, rows, height), jnp.bfloat16),
            pltpu.VMEM((16, rows, breadth), jnp.bfloat16),
            pltpu.VMEM((NE, height, breadth), jnp.bfloat16),
            pltpu.VMEM((height, breadth), jnp.float32),
            pltpu.VMEM((height, breadth), jnp.float32),
            pltpu.VMEM((6, NE, rows, breadth), jnp.float32),
            pltpu.VMEM((NE, 128, 128), jnp.float32),
            pltpu.VMEM((16, 8, 128), jnp.float32),
            pltpu.VMEM((16, 8, 128), jnp.float32),
            dma((3,)), dma((80,)), dma((32,)), dma((16,)),
            dma((16,)), dma((16,)), dma((16,)), dma((16,)),
        ],
        compiler_params=pltpu.CompilerParams(
            collective_id=0, has_side_effects=True, vmem_limit_bytes=60 * 1024 * 1024
        ),
    )(eps_static, eps_imag, frequency_grid, band_energy, pair)
    states = pair_elements.shape[1] // lax.axis_size(GCOL)
    return lax.dynamic_slice(summed, (0, lax.axis_index(GCOL) * states), (NE, states))


def solution(mesh):
    finer = Mesh(
        mesh.devices.reshape(2, 4, 2, 8, 2), ("grow_0", "grow_1", "grow_2", "gcol_0", "gcol_1")
    )
    in_specs = (P(GROW, GCOL), P(GROW, GCOL), P(), P(), P(GROW, None, GCOL))
    out_specs = P(None, GCOL)
    return jax.shard_map(
        shards, mesh=finer, in_specs=in_specs, out_specs=out_specs, check_vma=False
    )
```

time: 74 us -> 64.9 us (0.88)
  Pallas kernels: 72.5 us -> 63.5 us
    pallas_call x1, Pallas kernels: 72.5 us -> 63.5 us  [shards(): pl.pallas_call(kernel, out_shape=jax.ShapeDtypeStruct((8, 128), jnp.float...]
where the time goes in v3:
time: 64.9 us; the launch traced here: 64.8 us
  Pallas kernels  63.5 us (98%)
  local copies, waits for them, and re-layouts  1.34 us (2%)
    pallas_call x1, Pallas kernels, shards(): pl.pallas_call(kernel, out_shape=jax.ShapeDtypeStruct((8, 128), jnp.float...  63.5 us
    dynamic_slice x1, local copies, waits for them, and re-layouts, shards(): lax.dynamic_slice(summed, (0, lax.axis_index(GCOL) * states), (NE, states))  1.34 us

profile of v3, /device:TPU:1, one launch (start us, length us, event | category | flops | bytes accessed | tf_op | source)
XLA Modules:
  0.0 64.8 jit_solution(16793475258063952692)
XLA Ops:
  0.0 63.5 %shard_map.55 = f32[8,128]{1,0:T(8,128)} custom-call(f32[768,768]{1,0:T(8,128)} %static_hbm.1, f32[768,768]{1,0:T(8,128)} %imag_hbm.1, f32[3]{0:T(128)} %freq.1, f32[32]{0:T(128)} %band.1, bf16[128,768]{1,0:T(8,128)(2,1)} %bitcast.1), custom_call_target="tpu_custom_call" | custom-call | tf_op jit(solution)/shard_map/pallas_call | solution.py:298
  63.5 1.3 %constant_dynamic-slice_fusion = f32[3,4]{1,0:T(4,128)} fusion(f32[8,128]{1,0:T(8,128)} %shard_map.55, s32[]{:T(128)S(6)} %select_n.3), kind=kLoop, calls=%fused_computation | loop fusion | bytes 100 | tf_op jit(solution)/shard_map/dynamic_slice | solution.py:321

commit v4 on v3

--- a/solution.py
+++ b/solution.py
@@ -74,18 +74,22 @@
     def greet(device):
         pl.semaphore_signal(barrier, inc=1, device_id=device, device_id_type=MESH)
 
-    stays = jnp.logical_and(jnp.logical_and(plane == z, z == 0), core == yhi)
-    origin = lax.rem(z + plane, NZ)
+    stays = jnp.logical_and(jnp.logical_and(plane == z, z == 4 * core), core == yhi)
+    origin = lax.rem(z + 5 * plane + 4 * yhi, NZ)
 
     @pl.when(jnp.logical_not(stays))
     def _():
         greet((origin // NX, lax.rem(origin, NX), yhi, plane, core))
 
-    for device in along_z + in_plane:
+    across_y = (ylo, x, core, z, yhis[1])
+    beside_y = (ylos[1], x, core, z, yhi)
+    near = [beside_y, across_y, partner]
+    near += [(ylo, x, core, zs[i], yhi) for i in (1, -1)] + [(ylo, xs[i], core, z, yhi) for i in (1, 2, 3)]
+    for device in near:
         greet(device)
 
     loads[0].wait()
-    pl.semaphore_wait(barrier, 31 - stays.astype(jnp.int32))
+    pl.semaphore_wait(barrier, len(near) + 1 - stays.astype(jnp.int32))
 
     started = []
 
@@ -97,7 +101,7 @@
         started.append(copy)
         return copy
 
-    place = (z // NX, lax.rem(z, NX), yhi, lax.rem(plane + NZ - z, NZ), core)
+    place = (z // NX, lax.rem(z, NX), yhi, lax.rem(plane + 3 * z + 4 * core, NZ), core)
 
     def piece(panel, slot, part):
         return panel.at[slot, pl.ds(part * half, half)]
@@ -114,11 +118,13 @@
         for t in range(2):
             pltpu.make_async_copy(pair_hbm.at[pl.ds(t * half, half)], piece(rowp, row, t), row_recv.at[2 * row + t]).start()
 
-    pieces = {far: 2 * lax.rem(z + plane + 2 * NZ - far, NZ) for far in EVERY}
-    pieces[-4] = pieces[4]
+    starts = {
+        (chain, far): 2 * lax.rem(z + 5 * plane + 4 * yhis[chain] + NZ - far, NZ) + yhis[chain]
+        for chain in range(2) for far in EVERY
+    }
 
     def block(chain, far):
-        return pieces[far] + yhis[chain]
+        return starts[chain, 4 if far == -4 else far]
 
     arrived = set()
 
@@ -139,7 +145,7 @@
             pass_on(chain, way * far, part, (ylo, x, core, zs[way % NZ], yhi))
 
     def across(far, part):
-        pass_on(0, far, part, (ylo, x, core, z, yhis[1]))
+        pass_on(0, far, part, across_y)
 
     def col_slot(a, b, c):
         return 2 * (NX * a + b) + c
@@ -172,6 +178,7 @@
         return total
 
     kept = {}
+    places = [(e // 2, slice(e % 2 * half, (e % 2 + 1) * half)) for e in range(NE)]
 
     def rows_of(n):
         return slice(n * rowp.shape[1], (n + 1) * rowp.shape[1])
@@ -185,21 +192,21 @@
 
     def finish(keys):
         for e in range(NE):
-            total = acc[e, 0:half, :]
+            total = acc[places[e]]
             for key in keys:
                 total = total + weighted(ahead[kept[key], e], block(*key), e)
-            acc[e, 0:half, :] = total
+            acc[places[e]] = total
 
     def compute(keys):
         blocks = [block(*key) for key in keys]
         for e in range(NE):
             projected = project(blocks, e)
-            total = acc[e, 0:half, :]
+            total = acc[places[e]]
             for n, b in enumerate(blocks):
                 total = total + weighted(projected[rows_of(n)], b, e)
-            acc[e, 0:half, :] = total
-
-    col_send(row, (ylos[1], x, core, z, yhi))
+            acc[places[e]] = total
+
+    col_send(row, beside_y)
     col_send(row, partner)
     for dx in (1, 3, 2):
         col_send(row, (ylo, xs[dx], core, z, yhi))
@@ -248,36 +255,34 @@
             {"d": project_ahead, "m": finish, "c": compute}[op](args)
 
     ones = jnp.ones((8, 128), jnp.float32)
-    which = lax.broadcasted_iota(jnp.int32, (8, 128), 0)
-    tile = jnp.zeros((8, 128), jnp.float32)
-    for e in range(NE):
-        summed = lax.dot_general(
-            ones, acc[e], (((1,), (1,)), ((), ())),
+    tile = jnp.concatenate([
+        lax.dot_general(
+            ones, acc[i], (((1,), (1,)), ((), ())),
             precision=lax.Precision.HIGHEST, preferred_element_type=jnp.float32,
-        )
-        tile = tile + jnp.where(which == e, summed, 0.0)
+        )[0:1]
+        for i in range(2)
+    ])
 
     def exchange(buffer, me, value, devices, recv, sem):
         buffer[me] = value
         copies = [
             pltpu.make_async_remote_copy(
-                src_ref=buffer.at[me], dst_ref=buffer.at[me], send_sem=sem.at[i], recv_sem=recv.at[me],
+                src_ref=buffer.at[me], dst_ref=buffer.at[me], send_sem=sem.at[i], recv_sem=recv.at[0],
                 device_id=device, device_id_type=MESH,
             )
             for i, device in enumerate(devices)
         ]
         for copy in copies:
             copy.start()
-        for i in range(1, 16):
-            slot = lax.rem(me + i, 16)
-            pltpu.make_async_copy(buffer.at[slot], buffer.at[slot], recv.at[slot]).wait()
+        others = buffer.at[pl.ds(0, len(devices))]
+        pltpu.make_async_copy(others, others, recv.at[0]).wait()
         total = buffer[0]
         for i in range(1, 16):
             total = total + buffer[i]
         return total, copies
 
-    tile, last = exchange(red1, NX * (2 * yhi + ylo) + x, tile, in_plane, r1_recv, r1_send)
-    out[...], more = exchange(red2, 2 * z + core, tile, along_z, r2_recv, r2_send)
+    tile, last = exchange(red2, 2 * z + core, tile, along_z, r2_recv, r2_send)
+    out[...], more = exchange(red1, NX * (2 * yhi + ylo) + x, tile, in_plane, r1_recv, r1_send)
 
     @pl.when(jnp.logical_not(stays))
     def _():
@@ -297,7 +302,7 @@
     dma = pltpu.SemaphoreType.DMA
     summed = pl.pallas_call(
         kernel,
-        out_shape=jax.ShapeDtypeStruct((8, 128), jnp.float32),
+        out_shape=jax.ShapeDtypeStruct((2, 128), jnp.float32),
         in_specs=[anywhere, anywhere, scalars, scalars, anywhere],
         out_specs=pl.BlockSpec(memory_space=pltpu.VMEM),
         scratch_shapes=[
@@ -307,18 +312,18 @@
             pltpu.VMEM((height, breadth), jnp.float32),
             pltpu.VMEM((height, breadth), jnp.float32),
             pltpu.VMEM((6, NE, rows, breadth), jnp.float32),
-            pltpu.VMEM((NE, 128, 128), jnp.float32),
-            pltpu.VMEM((16, 8, 128), jnp.float32),
-            pltpu.VMEM((16, 8, 128), jnp.float32),
+            pltpu.VMEM((2, 128, 128), jnp.float32),
+            pltpu.VMEM((16, 2, 128), jnp.float32),
+            pltpu.VMEM((16, 2, 128), jnp.float32),
             dma((3,)), dma((80,)), dma((32,)), dma((16,)),
-            dma((16,)), dma((16,)), dma((16,)), dma((16,)),
+            dma((1,)), dma((15,)), dma((1,)), dma((15,)),
         ],
         compiler_params=pltpu.CompilerParams(
             collective_id=0, has_side_effects=True, vmem_limit_bytes=60 * 1024 * 1024
         ),
     )(eps_static, eps_imag, frequency_grid, band_energy, pair)
     states = pair_elements.shape[1] // lax.axis_size(GCOL)
-    return lax.dynamic_slice(summed, (0, lax.axis_index(GCOL) * states), (NE, states))
+    return lax.dynamic_slice(summed.reshape(4, 64), (0, lax.axis_index(GCOL) * states), (NE, states))
 
 
 def solution(mesh):

time: 64.9 us -> 62.4 us (0.961)
  Pallas kernels: 63.5 us -> 60.8 us
    pallas_call x1, Pallas kernels: 63.5 us -> 60.8 us  [shards(): pl.pallas_call(kernel, out_shape=jax.ShapeDtypeStruct((2, 128), jnp.float...]
    reshape x0 -> x1, local copies, waits for them, and re-layouts: none -> 0.76 us  [shards(): summed.reshape(4, 64)]
    dynamic_slice x1, local copies, waits for them, and re-layouts: 1.34 us -> 0.65 us  [shards(): lax.dynamic_slice(summed.reshape(4, 64), (0, lax.axis_index(GCOL) * state...]
where the time goes in v4:
time: 62.4 us; the launch traced here: 62.3 us
  Pallas kernels  60.8 us (97%)
  local copies, waits for them, and re-layouts  1.41 us (2%)
    pallas_call x1, Pallas kernels, shards(): pl.pallas_call(kernel, out_shape=jax.ShapeDtypeStruct((2, 128), jnp.float...  60.8 us

profile of v4, /device:TPU:1, one launch (start us, length us, event | category | flops | bytes accessed | tf_op | source)
XLA Modules:
  0.0 62.3 jit_solution(8611850948567166599)
XLA Ops:
  0.0 60.8 %shard_map.55 = f32[2,128]{1,0:T(2,128)} custom-call(f32[768,768]{1,0:T(8,128)} %static_hbm.1, f32[768,768]{1,0:T(8,128)} %imag_hbm.1, f32[3]{0:T(128)} %freq.1, f32[32]{0:T(128)} %band.1, bf16[128,768]{1,0:T(8,128)(2,1)} %bitcast.1), custom_call_target="tpu_custom_call" | custom-call | tf_op jit(solution)/shard_map/pallas_call | solution.py:303
  60.8 0.8 %reshape.7 = f32[4,64]{1,0:T(4,128)S(1)} reshape(f32[2,128]{1,0:T(2,128)} %shard_map.55) | data formatting | bytes 2048 | tf_op jit(solution)/shard_map/reshape | solution.py:326
  61.6 0.7 %constant_dynamic-slice_fusion = f32[3,4]{1,0:T(4,128)} fusion(f32[4,64]{1,0:T(4,128)S(1)} %reshape.7, s32[]{:T(128)S(6)} %select_n.3), kind=kLoop, calls=%fused_computation | loop fusion | bytes 100 | tf_op jit(solution)/shard_map/dynamic_slice | solution.py:326

commit v5 on v4

--- a/solution.py
+++ b/solution.py
@@ -14,28 +14,69 @@
 MESH = pl.DeviceIdType.MESH
 SLICE = 16
 EVERY = (0, 1, -1, 2, -2, 3, -3, 4)
+PARTS = 4
 PROGRAM = (
     ("n",),
-    ("z", 0, 0, 0), ("y", 0, 0),
-    ("r", 0), ("r", 1),
-    ("z", 0, 0, 1), ("y", 0, 1), ("z", 0, 1, 0), ("y", 1, 0),
+    ("z", 0, 0, 0),
+    ("y", 0, 0),
+    ("z", 0, 0, 1),
+    ("y", 0, 1),
+    ("z", 0, 1, 0),
+    ("y", 1, 0),
+    ("y", -1, 0),
+    ("z", 0, 0, 2),
+    ("z", 0, 1, 1),
+    ("y", 1, 1),
+    ("r", 0),
+    ("r", 1),
+    ("y", -1, 1),
+    ("z", 0, 0, 3),
+    ("z", 0, 2, 0),
+    ("y", 0, 2),
+    ("z", 0, 1, 2),
+    ("y", 1, 2),
     ("r", 2),
-    ("y", -1, 0), ("z", 0, 1, 1), ("y", 1, 1),
-    ("d", (0, 0), (1, 0)),
-    ("z", 0, 2, 0),
+    ("z", 0, 2, 1),
+    ("y", 2, 1),
+    ("y", -2, 1),
+    ("z", 0, 1, 3),
+    ("d", (0, 1), (0, -1)),
     ("r", 3),
-    ("y", -1, 1), ("z", 0, 2, 1),
-    ("d", (0, 1), (0, -1)),
-    ("z", 1, 1, 0), ("r", 4), ("y", 3, 1), ("z", 0, 3, 0), ("z", 0, 3, 1),
+    ("y", 3, 0),
+    ("z", 1, 1, 0),
+    ("y", -3, 0),
+    ("z", 0, 2, 2),
+    ("y", -1, 2),
+    ("z", 0, 2, 3),
+    ("r", 4),
+    ("y", 0, 3),
+    ("z", 1, 2, 1),
     ("d", (0, 2), (0, -2)),
-    ("y", -3, 1), ("z", 1, 1, 1),
-    ("r", 5), ("y", 4, 0), ("z", 1, 2, 0),
+    ("y", 1, 3),
+    ("r", 5),
+    ("z", 0, 3, 0),
+    ("z", 0, 3, 2),
+    ("y", -1, 3),
+    ("z", 0, 3, 1),
+    ("z", 0, 3, 3),
     ("w",),
+    ("y", 3, 3),
+    ("z", 1, 1, 2),
+    ("c", (0, 3), (0, -3)),
+    ("y", -3, 3),
+    ("z", 1, 3, 1),
+    ("y", 4, 0),
+    ("c", (0, 0), (1, 0)),
+    ("y", 4, 2),
+    ("z", 1, 1, 3),
+    ("c", (0, 4)),
+    ("y", 4, 3),
+    ("z", 1, 2, 2),
+    ("m", (0, 1), (0, -1), (0, 2), (0, -2)),
     ("c", (1, 1), (1, -1)),
-    ("z", 1, 3, 1),
-    ("c", (0, 3), (0, -3)),
-    ("m", (0, 0), (1, 0), (0, 1), (0, -1), (0, 2), (0, -2)),
-    ("c", (0, 4),), ("c", (1, 2), (1, -2)), ("c", (1, 3), (1, -3)), ("c", (1, 4),),
+    ("c", (1, 2), (1, -2)),
+    ("c", (1, 3), (1, -3)),
+    ("c", (1, 4)),
 )
 
 
@@ -50,6 +91,7 @@
     row = plane * 2 + core
     col = z * 2 + yhi
     half = rowp.shape[1] // 2
+    share = rowp.shape[1] // PARTS
     partner = (ylo, x, 1 - core, z, yhi)
     xs = [lax.rem(x + i, NX) for i in range(NX)]
     zs = [lax.rem(z + i, NZ) for i in range(NZ)]
@@ -104,9 +146,9 @@
     place = (z // NX, lax.rem(z, NX), yhi, lax.rem(plane + 3 * z + 4 * core, NZ), core)
 
     def piece(panel, slot, part):
-        return panel.at[slot, pl.ds(part * half, half)]
-
-    first = [send(piece(colp, row, t), piece(rowp, row, t), row_recv.at[2 * row + t], place) for t in range(2)]
+        return panel.at[slot, pl.ds(part * share, share)]
+
+    first = [send(piece(colp, row, t), piece(rowp, row, t), row_recv.at[PARTS * row + t], place) for t in range(PARTS)]
 
     @pl.when(jnp.logical_not(stays))
     def _():
@@ -115,8 +157,8 @@
 
     @pl.when(stays)
     def _():
-        for t in range(2):
-            pltpu.make_async_copy(pair_hbm.at[pl.ds(t * half, half)], piece(rowp, row, t), row_recv.at[2 * row + t]).start()
+        for t in range(PARTS):
+            pltpu.make_async_copy(pair_hbm.at[pl.ds(t * share, share)], piece(rowp, row, t), row_recv.at[PARTS * row + t]).start()
 
     starts = {
         (chain, far): 2 * lax.rem(z + 5 * plane + 4 * yhis[chain] + NZ - far, NZ) + yhis[chain]
@@ -133,15 +175,15 @@
         if (chain, far, part) not in arrived:
             arrived.add((chain, far, part))
             b = block(chain, far)
-            pltpu.make_async_copy(piece(rowp, b, part), piece(rowp, b, part), row_recv.at[2 * b + part]).wait()
+            pltpu.make_async_copy(piece(rowp, b, part), piece(rowp, b, part), row_recv.at[PARTS * b + part]).wait()
 
     def pass_on(chain, far, part, device):
         need(chain, far, part)
         b = block(chain, far)
-        send(piece(rowp, b, part), piece(rowp, b, part), row_recv.at[2 * b + part], device).start()
+        send(piece(rowp, b, part), piece(rowp, b, part), row_recv.at[PARTS * b + part], device).start()
 
     def along(chain, far, part):
-        for way in (1, -1) if far < 3 else ((1,) if part == 0 else (-1,)):
+        for way in (1, -1) if far < 3 else ((1,) if part < PARTS // 2 else (-1,)):
             pass_on(chain, way * far, part, (ylo, x, core, zs[way % NZ], yhi))
 
     def across(far, part):
@@ -250,8 +292,8 @@
                     col_wait(col_slot(a, b, 1 - core))
         else:
             for chain, far in args:
-                need(chain, far, 0)
-                need(chain, far, 1)
+                for part in range(PARTS):
+                    need(chain, far, part)
             {"d": project_ahead, "m": finish, "c": compute}[op](args)
 
     ones = jnp.ones((8, 128), jnp.float32)
@@ -289,7 +331,7 @@
         for copy in first:
             copy.wait_send()
 
-    for copy in started[2:] + last + more:
+    for copy in started[PARTS:] + last + more:
         copy.wait_send()
 
 
@@ -311,11 +353,11 @@
             pltpu.VMEM((NE, height, breadth), jnp.bfloat16),
             pltpu.VMEM((height, breadth), jnp.float32),
             pltpu.VMEM((height, breadth), jnp.float32),
-            pltpu.VMEM((6, NE, rows, breadth), jnp.float32),
+            pltpu.VMEM((4, NE, rows, breadth), jnp.float32),
             pltpu.VMEM((2, 128, 128), jnp.float32),
             pltpu.VMEM((16, 2, 128), jnp.float32),
             pltpu.VMEM((16, 2, 128), jnp.float32),
-            dma((3,)), dma((80,)), dma((32,)), dma((16,)),
+            dma((3,)), dma((128,)), dma((16 * PARTS,)), dma((16,)),
             dma((1,)), dma((15,)), dma((1,)), dma((15,)),
         ],
         compiler_params=pltpu.CompilerParams(

time: 62.4 us -> 61.7 us (0.989)
  Pallas kernels: 60.8 us -> 60.1 us
    pallas_call x1, Pallas kernels: 60.8 us -> 60.1 us  [shards(): pl.pallas_call(kernel, out_shape=jax.ShapeDtypeStruct((2, 128), jnp.float...]
where the time goes in v5:
time: 61.7 us; the launch traced here: 61.6 us
  Pallas kernels  60.1 us (97%)
  local copies, waits for them, and re-layouts  1.41 us (2%)
    pallas_call x1, Pallas kernels, shards(): pl.pallas_call(kernel, out_shape=jax.ShapeDtypeStruct((2, 128), jnp.float...  60.1 us

profile of v5, /device:TPU:1, one launch (start us, length us, event | category | flops | bytes accessed | tf_op | source)
XLA Modules:
  0.0 61.6 jit_solution(13111322506301857398)
XLA Ops:
  0.0 60.1 %shard_map.55 = f32[2,128]{1,0:T(2,128)} custom-call(f32[768,768]{1,0:T(8,128)} %static_hbm.1, f32[768,768]{1,0:T(8,128)} %imag_hbm.1, f32[3]{0:T(128)} %freq.1, f32[32]{0:T(128)} %band.1, bf16[128,768]{1,0:T(8,128)(2,1)} %bitcast.1), custom_call_target="tpu_custom_call" | custom-call | tf_op jit(solution)/shard_map/pallas_call | solution.py:345
  60.1 0.8 %reshape.7 = f32[4,64]{1,0:T(4,128)S(1)} reshape(f32[2,128]{1,0:T(2,128)} %shard_map.55) | data formatting | bytes 2048 | tf_op jit(solution)/shard_map/reshape | solution.py:368
  60.9 0.7 %constant_dynamic-slice_fusion = f32[3,4]{1,0:T(4,128)} fusion(f32[4,64]{1,0:T(4,128)S(1)} %reshape.7, s32[]{:T(128)S(6)} %select_n.3), kind=kLoop, calls=%fused_computation | loop fusion | bytes 100 | tf_op jit(solution)/shard_map/dynamic_slice | solution.py:368
